TPU v7x, 512 devices: a whole 4x8x8 slice. The times are simulated.
512 devices in a mesh: replica: 16 (over z, core), mp: 16 (over y, x_hi), refresh: 2 (over x_lo).
Axes of the slice: x: 4 (x_hi: 2, x_lo: 2; x = x_hi * 2 + x_lo), y: 8, z: 8, core: 2. Of those that a mesh axis runs over, the one named last changes fastest.
Arguments:
- grad_partial: bfloat16 [16, 2, 512, 8192], P('replica', 'refresh', 'mp'), may hold values from -63 to 63
- left_stats: float32 [2, 512, 8192], P('refresh', 'replica', 'mp'), may hold values from -4608 to 5120, as said below
- right_stats: float32 [2, 512, 8192], P('refresh', 'replica', 'mp'), may hold values from -4608 to 5120, as said below
- left_roots: float32 [2, 512, 8192], P('refresh', 'replica', 'mp'), may hold values from -1 to 1, as said below
- right_roots: float32 [2, 512, 8192], P('refresh', 'replica', 'mp'), may hold values from -1 to 1, as said below
- newton_counts: int32 [2, 16], replicated, may hold values from 1 to 4
- owner: int32 [2, 16], replicated, may hold values from 0 to 15, each once within a row
Outputs:
- update: float32 [2, 512, 8192], P('refresh', 'mp')
- new_left_stats: float32 [2, 512, 8192], P('refresh', 'replica', 'mp')
- new_right_stats: float32 [2, 512, 8192], P('refresh', 'replica', 'mp')
- new_left_roots: float32 [2, 512, 8192], P('refresh', 'replica', 'mp')
- new_right_roots: float32 [2, 512, 8192], P('refresh', 'replica', 'mp')
Inputs may be any that keep to these rules, and one draw needn't show every extreme that they name: Each row of owner names every owner index once. `left_stats`: every 512 x 512 block is symmetric positive definite. `right_stats`: every 512 x 512 block is symmetric positive definite. `left_roots`: every 512 x 512 block is symmetric. `right_roots`: every 512 x 512 block is symmetric.
All inputs are finite; a program needn't handle non-finite values.
Results may differ from a plain program's by a relative error of at most 0.0003.
Values may be sent and summed in bfloat16 or wider, within the bound.
No kernel may reach another device: no remote copies, remote signals or barrier semaphores. Data moves between devices by JAX's collectives and lax.ppermute only.
A program may use at most 64 MiB of HBM per device.

v0:
```python
import functools
import jax
import jax.numpy as jnp
from jax import lax
from jax.sharding import Mesh
from jax.sharding import PartitionSpec as P

MP = ("mp_0", "mp_1")
REPLICA = ("replica_0", "replica_1")
REPLICA_MP_REFRESH = ("replica_0", "replica_1", "mp_0", "mp_1", "refresh")
decay = 0.9
graft_eps = 1e-06


def split_up(shard, dim, count):
    before, after = (shard.shape[:dim], shard.shape[dim + 1 :])
    return jnp.moveaxis(shard.reshape(*before, count, -1, *after), dim, 0)


def summed_on_arrival(shard, axis, dim):
    tiles = split_up(shard, dim, lax.axis_size(axis))
    arrived = lax.all_to_all(tiles, axis, split_axis=0, concat_axis=0, tiled=True)
    return arrived.sum(axis=0)


def by_axis(shard, axes):
    return functools.reduce(lax.psum, axes, shard)


def side_by_side(arrays, axis, dim, along):
    widths = [a.shape[along] for a in arrays]
    both = jnp.concatenate(arrays, axis=along)
    filled = lax.all_gather(both, axis, axis=dim, tiled=True)
    return tuple(jnp.split(filled, [sum(widths[:k]) for k in range(1, len(widths))], axis=along))


def swapped(shard, axis, stride):
    return lax.ppermute(shard, axis, [(i, i ^ 1 << stride) for i in range(lax.axis_size(axis))])


def sent_to_all(shard, axis):
    count = lax.axis_size(axis)
    return lax.all_to_all(
        jnp.broadcast_to(shard[None], (count, *shard.shape)), axis, 0, 0, tiled=True
    )


def laid_out(tiles, dim):
    lengths = list(tiles.shape[1:])
    lengths[dim] *= tiles.shape[0]
    return jnp.moveaxis(tiles, 0, dim).reshape(lengths)


def gather_directly(shard, axis, dim):
    tiles = sent_to_all(shard, axis)
    return laid_out(tiles, dim)


def product(left, right):
    return jnp.dot(left, right, precision=lax.Precision.HIGHEST, preferred_element_type=jnp.float32)


def newton_step(iterate, coupled, coupled_full, eye):
    factor = (5.0 * eye - coupled_full) * 0.25
    next_iterate = product(iterate, factor)
    next_coupled = product(product(product(product(coupled, factor), factor), factor), factor)
    return (next_iterate, next_coupled)


def run_iterations(advance, state, count):
    return lax.fori_loop(0, count, advance, state)


def make_folder(grad_rows, left_slab, replica_index, rows_rep):

    def fold_rows(carry, piece, start):
        left_acc = product(grad_rows, piece.T)
        own_cols = lax.dynamic_slice_in_dim(piece, replica_index * rows_rep, rows_rep, 1)
        right_acc = product(own_cols.T, piece)
        half_acc = product(left_slab, piece)
        return (left_acc, right_acc, half_acc)

    return fold_rows


def local(grad_partial, left_stats, right_stats, left_roots, right_roots, newton_counts, owner):
    group = lax.axis_index("refresh")
    owner_index = lax.axis_index(MP)
    replica_index = lax.axis_index(REPLICA)
    owners = lax.axis_size(MP)
    replicas = lax.axis_size(REPLICA)
    rows_part = grad_partial[0, 0]
    rows_mp = rows_part.shape[0]
    order = rows_part.shape[1] // owners
    rows_rep = order // replicas
    owner_row = lax.dynamic_index_in_dim(owner, group, 0, keepdims=False)
    counts_row = lax.dynamic_index_in_dim(newton_counts, group, 0, keepdims=False)
    slots = jnp.arange(owners, dtype=jnp.int32)
    hits = owner_row[:, None] == slots[None, :]
    inverse = jnp.sum(jnp.where(hits, slots[:, None], 0), axis=0)
    count = jnp.sum(jnp.where(owner_row == owner_index, counts_row, 0))
    ordered = jnp.take(rows_part.reshape(rows_mp, owners, order), inverse, axis=1).reshape(
        rows_mp, owners * order
    )
    left_slab = left_roots[0]
    right_slab = right_roots[0]
    zeros = jnp.zeros((rows_rep, order), jnp.float32)
    routed = lax.all_to_all(ordered, MP, split_axis=1, concat_axis=0, tiled=True)
    grad_rows = summed_on_arrival(routed.astype(jnp.float32), REPLICA, 0)
    folder = make_folder(grad_rows, left_slab, replica_index, rows_rep)
    left_term, right_term, half_dir = folder(
        (zeros, zeros, zeros), lax.all_gather(grad_rows, REPLICA, axis=0, tiled=True), jnp.int32(0)
    )
    direction = product(half_dir, lax.all_gather(right_slab, REPLICA, axis=0, tiled=True))
    new_left = decay * left_stats[0] + (1.0 - decay) * left_term
    new_right = decay * right_stats[0] + (1.0 - decay) * right_term
    grad_sq, dir_sq = (
        by_axis(jnp.sum(grad_rows * grad_rows), REPLICA_MP_REFRESH),
        by_axis(jnp.sum(direction * direction), REPLICA_MP_REFRESH),
    )
    scaled = direction * (jnp.sqrt(grad_sq) / jnp.sqrt(dir_sq + graft_eps))
    eye = jnp.eye(order, dtype=jnp.float32)
    left_full, right_full = side_by_side((new_left, new_right), REPLICA, 0, 1)
    parity = replica_index % 2
    chosen = jnp.where(parity == 0, left_full, right_full)
    scale = 2.5 / jnp.sqrt(jnp.sum(chosen * chosen))
    state = (scale**0.25 * eye, scale * chosen)

    def advance_whole(step_index, current):
        return newton_step(current[0], current[1], current[1], eye)

    iterate = run_iterations(advance_whole, state, count)[0]
    partner = replica_index + 1 - 2 * parity
    outgoing = lax.dynamic_slice_in_dim(iterate, partner * rows_rep, rows_rep, 0)
    incoming = swapped(outgoing, REPLICA, 0)
    own_rows = lax.dynamic_slice_in_dim(iterate, replica_index * rows_rep, rows_rep, 0)
    left_root = jnp.where(parity == 0, own_rows, incoming)
    right_root = jnp.where(parity == 0, incoming, own_rows)
    whole_update = gather_directly(scaled, REPLICA, 0)
    returned = lax.all_to_all(whole_update, MP, split_axis=0, concat_axis=1, tiled=True)
    update = jnp.take(returned.reshape(rows_mp, owners, order), owner_row, axis=1).reshape(
        1, rows_mp, owners * order
    )
    return (update, new_left[None], new_right[None], left_root[None], right_root[None])


def solution(mesh):
    finer = Mesh(
        mesh.devices.reshape(8, 2, 8, 2, mesh.shape["refresh"]),
        ("replica_0", "replica_1", "mp_0", "mp_1", "refresh"),
    )
    in_specs = (
        P(REPLICA, "refresh", MP, None),
        P("refresh", REPLICA, MP),
        P("refresh", REPLICA, MP),
        P("refresh", REPLICA, MP),
        P("refresh", REPLICA, MP),
        P(),
        P(),
    )
    out_specs = (
        P("refresh", MP, None),
        P("refresh", REPLICA, MP),
        P("refresh", REPLICA, MP),
        P("refresh", REPLICA, MP),
        P("refresh", REPLICA, MP),
    )
    return jax.shard_map(local, mesh=finer, in_specs=in_specs, out_specs=out_specs, check_vma=False)
```

profile of v0, /device:TPU:1, one launch (start us, length us, event | category | flops | bytes accessed | tf_op | source)
XLA Modules:
  0.0 316.1 jit_solution(1481063598009808224)
XLA Ops:
  7.2 1.4 fusion.54
  8.7 1.2 copy.25
  10.9 27.2 %all_to_all.33 = bf16[32,16,512]{2,0,1:T(8,128)(2,1)S(1)} all-to-all(bf16[32,16,512]{2,0,1:T(8,128)(2,1)S(1)} %select_bitcast_fusion), channel_id=1, replica_groups=mesh['replica_0'=8,'replica_1'=2,'mp_0'=8,'mp_1'=2,'refresh'=2] {'mp_0',..., dimensions={1} | all-to-all | bytes 1048576 | tf_op jit(solution)/shard_map/all_to_all | solution.py:108
  38.3 41.3 %all_to_all.34 = f32[16,32,512]{2,1,0:T(8,128)S(1)} all-to-all(f32[16,32,512]{2,1,0:T(8,128)S(1)} %convert_bitcast_fusion), channel_id=1, replica_groups=mesh['replica_0'=8,'replica_1'=2,'mp_0'=8,'mp_1'=2,'refresh'=2] {'replic..., dimensions={0} | all-to-all | bytes 2097152 | tf_op jit(solution)/shard_map/all_to_all | solution.py:22
  79.5 0.7 reduce_sum.58
  80.3 0.7 all-gather.9.cloned.1.call-update
  81.1 31.6 %all-gather.5.cloned.1.call-done = f32[512,512]{1,0:T(8,128)} async-done(((f32[32,512]{1,0:T(8,128)}), f32[512,512]{1,0:T(8,128)}) %all-gather.5.cloned.1.call-update) | async-done | bytes 1048592 | tf_op jit(solution)/shard_map/all_gather | solution.py:112
  112.6 2.1 fusion.43
  114.8 2.3 fusion.42
  117.1 0.7 pad_maximum_fusion
  118.5 0.7 fusion.48
  119.2 35.6 %all-gather.9.cloned.1.call-done = f32[1,512,512]{2,1,0:T(8,128)} async-done(((f32[1,32,512]{2,1,0:T(8,128)}), f32[1,512,512]{2,1,0:T(8,128)}) %all-gather.9.cloned.1.call-update) | async-done | bytes 1048592 | tf_op jit(solution)/shard_map/all_gather | solution.py:114
  154.8 2.5 multiply_reduce_fusion.1
  157.3 12.4 %all-reduce.1 = (f32[]{:T(128)}, f32[]{:T(128)}) all-reduce(f32[]{:T(128)} %multiply_reduce_fusion.2, f32[]{:T(128)} %get-tuple-element.67), channel_id=1, replica_groups=mesh['replica_0'=8,'replica_1'=2,'mp_0'=8,'mp_1'=2,'refresh'=2] {'replic..., use_global_device_ids=true, to_apply=%region_3.4 | all-reduce | flops 2 | bytes 16 | tf_op jit(solution)/shard_map/psum | solution.py:27
  169.7 6.8 %all-reduce.4 = (f32[]{:T(128)}, f32[]{:T(128)}) all-reduce(f32[]{:T(128)} %get-tuple-element.55, f32[]{:T(128)} %get-tuple-element.56), channel_id=1, replica_groups=mesh['replica_0'=8,'replica_1'=2,'mp_0'=8,'mp_1'=2,'refresh'=2] {'replic..., use_global_device_ids=true, to_apply=%region_4.5 | all-reduce | flops 2 | bytes 16 | tf_op jit(solution)/shard_map/psum | solution.py:27
  176.5 14.4 %all-reduce = (f32[]{:T(128)}, f32[]{:T(128)}) all-reduce(f32[]{:T(128)} %get-tuple-element.61, f32[]{:T(128)} %get-tuple-element.62), channel_id=1, replica_groups=mesh['replica_0'=8,'replica_1'=2,'mp_0'=8,'mp_1'=2,'refresh'=2] {'mp_0'}, use_global_device_ids=true, to_apply=%region_5.6 | all-reduce | flops 2 | bytes 16 | tf_op jit(solution)/shard_map/psum | solution.py:27
  191.0 6.0 %all-reduce.3 = (f32[]{:T(128)}, f32[]{:T(128)}) all-reduce(f32[]{:T(128)} %get-tuple-element.53, f32[]{:T(128)} %get-tuple-element.54), channel_id=1, replica_groups=mesh['replica_0'=8,'replica_1'=2,'mp_0'=8,'mp_1'=2,'refresh'=2] {'mp_1'}, use_global_device_ids=true, to_apply=%region_6.7 | all-reduce | flops 2 | bytes 16 | tf_op jit(solution)/shard_map/psum | solution.py:27
  196.9 4.4 %all-reduce.2 = (f32[]{:T(128)}, f32[]{:T(128)}) all-reduce(f32[]{:T(128)} %get-tuple-element.59, f32[]{:T(128)} %get-tuple-element.60), channel_id=1, replica_groups=mesh['replica_0'=8,'replica_1'=2,'mp_0'=8,'mp_1'=2,'refresh'=2] {'refresh'}, use_global_device_ids=true, to_apply=%region_7.8 | all-reduce | flops 2 | bytes 16 | tf_op jit(solution)/shard_map/psum | solution.py:27
  202.7 1.1 broadcast_in_dim.66
  203.8 11.0 %all-to-all-start.2 = ((f32[16,32,512]{2,1,0:T(8,128)}), f32[16,32,512]{2,1,0:T(8,128)}, u32[]{:S(2)}, u32[]{:S(2)}) async-start(f32[16,32,512]{2,1,0:T(8,128)} %broadcast_in_dim.66), calls=%async_computation.2 | async-start | bytes 2097152 | tf_op jit(solution)/shard_map/all_to_all | solution.py:43
  215.0 28.0 %all-to-all-done.2 = f32[16,32,512]{2,1,0:T(8,128)} async-done(((f32[16,32,512]{2,1,0:T(8,128)}), f32[16,32,512]{2,1,0:T(8,128)}, u32[]{:S(2)}, u32[]{:S(2)}) %all-to-all-start.2) | async-done | bytes 1048608 | tf_op jit(solution)/shard_map/all_to_all | solution.py:43
  242.9 6.7 %all-to-all-start.3 = ((f32[16,32,512]{2,1,0:T(8,128)}), f32[16,32,512]{2,1,0:T(8,128)S(1)}, u32[]{:S(2)}, u32[]{:S(2)}) async-start(f32[16,32,512]{2,1,0:T(8,128)} %all-to-all-done.2), calls=%async_computation.3 | async-start | bytes 2097152 | tf_op jit(solution)/shard_map/all_to_all | solution.py:140
  249.7 2.4 multiply_reduce_fusion
  253.0 1.8 broadcast_multiply_fusion
  254.7 48.5 %while.13 = (s32[]{:T(128)}, f32[512,512]{0,1:T(8,128)S(1)}, f32[512,512]{1,0:T(8,128)S(1)}, s32[]{:T(128)}, s32[]{:T(128)}) while((s32[]{:T(128)}, f32[512,512]{0,1:T(8,128)S(1)}, f32[512,512]{1,0:T(8,128)S(1)}, s32[]{:T(128)}, s32[]{:T(128)}) %tuple.29), condition=%wide.region_17.18_spmd.clone, body=%wide.region_16.17_spmd.clone.sunk | while | flops 8058306560 | bytes 18874428 | solution.py:71
  255.7 3.5 %fusion.91 = f32[512,512]{1,0:T(8,128)S(1)} fusion(f32[512,512]{1,0:T(8,128)S(1)} %copy.39), kind=kOutput, calls=%fused_computation.10.clone.1 | convolution fusion | flops 1611661312 | bytes 2097152 | tf_op jit(solution)/shard_map/while/body/dot_general | solution.py:60
  259.2 1.9 fusion.92
  261.1 1.9 fusion.93
  263.0 1.9 convolution_bitcast_fusion.2
  264.9 1.9 fusion.94
  267.6 3.5 %fusion.91 = f32[512,512]{1,0:T(8,128)S(1)} fusion(f32[512,512]{1,0:T(8,128)S(1)} %copy.39), kind=kOutput, calls=%fused_computation.10.clone.1 | convolution fusion | flops 1611661312 | bytes 2097152 | tf_op jit(solution)/shard_map/while/body/dot_general | solution.py:60
  271.1 1.9 fusion.92
  273.0 1.9 fusion.93
  275.0 1.9 convolution_bitcast_fusion.2
  276.9 1.9 fusion.94
  279.6 3.5 %fusion.91 = f32[512,512]{1,0:T(8,128)S(1)} fusion(f32[512,512]{1,0:T(8,128)S(1)} %copy.39), kind=kOutput, calls=%fused_computation.10.clone.1 | convolution fusion | flops 1611661312 | bytes 2097152 | tf_op jit(solution)/shard_map/while/body/dot_general | solution.py:60
  283.1 1.9 fusion.92
  285.0 1.9 fusion.93
  286.9 1.9 convolution_bitcast_fusion.2
  288.8 1.9 fusion.94
  291.5 3.5 %fusion.91 = f32[512,512]{1,0:T(8,128)S(1)} fusion(f32[512,512]{1,0:T(8,128)S(1)} %copy.39), kind=kOutput, calls=%fused_computation.10.clone.1 | convolution fusion | flops 1611661312 | bytes 2097152 | tf_op jit(solution)/shard_map/while/body/dot_general | solution.py:60
  295.0 1.9 fusion.92
  296.9 1.9 fusion.93
  298.8 1.9 convolution_bitcast_fusion.2
  300.7 1.9 fusion.94
  303.7 1.9 collective-permute-start
  307.0 1.1 broadcast_select_fusion
  308.1 1.5 select_bitcast_fusion.1
  (54 shorter events, 4.6 us)
Async XLA Ops:
  7.2 111.3 %copy-start = (f32[1,32,512]{2,1,0:T(8,128)S(1)}, f32[1,32,512]{2,1,0:T(8,128)}, u32[]{:S(2)}) copy-start(f32[1,32,512]{2,1,0:T(8,128)} %param.12) | copy-start | bytes 196612
  7.2 105.5 %all-gather.5.cloned.1.call-start = ((), (), s32[]{:S(2)}) async-start(), calls=%async_computation.4 | async-start | bytes 1114112 | tf_op jit(solution)/shard_map/all_gather | solution.py:112
  38.1 74.5 %copy-start.6 = (f32[1,32,512]{2,1,0:T(8,128)S(1)}, f32[1,32,512]{2,1,0:T(8,128)}, u32[]{:S(2)}) copy-start(f32[1,32,512]{2,1,0:T(8,128)} %param.11) | copy-start | bytes 196612
  38.3 76.5 %copy-start.7 = (f32[1,32,512]{2,1,0:T(8,128)S(1)}, f32[1,32,512]{2,1,0:T(8,128)}, u32[]{:S(2)}) copy-start(f32[1,32,512]{2,1,0:T(8,128)} %param.10) | copy-start | bytes 196612
  80.2 37.6 %copy-start.3 = (f32[32,512]{1,0:T(8,128)S(1)}, f32[32,512]{1,0:T(8,128)}, u32[]{:S(2)}) copy-start(f32[32,512]{1,0:T(8,128)} %reduce_sum.58) | copy-start | bytes 196612
  80.3 74.5 %all-gather.9.cloned.1.call-start = ((), (), s32[]{:S(2)}) async-start(), calls=%async_computation.6 | async-start | bytes 1114112 | tf_op jit(solution)/shard_map/all_gather | solution.py:114
  81.0 168.7 %all-gather.7.cloned.1.call-start = ((), (), s32[]{:S(2)}) async-start(), calls=%async_computation.5 | async-start | bytes 2228224 | tf_op jit(solution)/shard_map/all_gather | solution.py:33
  112.6 5.8 %copy-start.1 = (f32[512,512]{1,0:T(8,128)S(1)}, f32[512,512]{1,0:T(8,128)}, u32[]{:S(2)}) copy-start(f32[512,512]{1,0:T(8,128)} %all-gather.5.cloned.1.call-done) | copy-start | bytes 3145732
  114.8 87.9 %copy-start.4 = (f32[32,512]{1,0:T(8,128)}, f32[32,512]{1,0:T(8,128)S(1)}, u32[]{:S(2)}) copy-start(f32[32,512]{1,0:T(8,128)S(1)} %fusion.43) | copy-start | bytes 196612
  117.1 86.7 %copy-start.5 = (f32[32,512]{1,0:T(8,128)}, f32[32,512]{1,0:T(8,128)S(1)}, u32[]{:S(2)}) copy-start(f32[32,512]{1,0:T(8,128)S(1)} %fusion.42) | copy-start | bytes 196612
  119.2 95.7 %copy-start.8 = (s32[2,16]{1,0:T(2,128)S(1)}, s32[2,16]{1,0:T(2,128)}, u32[]{:S(2)}) copy-start(s32[2,16]{1,0:T(2,128)} %param.15) | copy-start | bytes 388
  203.8 39.1 %all-to-all-start.2 = ((f32[16,32,512]{2,1,0:T(8,128)}), f32[16,32,512]{2,1,0:T(8,128)}, u32[]{:S(2)}, u32[]{:S(2)}) async-start(f32[16,32,512]{2,1,0:T(8,128)} %broadcast_in_dim.66), calls=%async_computation.2 | async-start | bytes 2097152 | tf_op jit(solution)/shard_map/all_to_all | solution.py:43
  242.9 62.7 %all-to-all-start.3 = ((f32[16,32,512]{2,1,0:T(8,128)}), f32[16,32,512]{2,1,0:T(8,128)S(1)}, u32[]{:S(2)}, u32[]{:S(2)}) async-start(f32[16,32,512]{2,1,0:T(8,128)} %all-to-all-done.2), calls=%async_computation.3 | async-start | bytes 2097152 | tf_op jit(solution)/shard_map/all_to_all | solution.py:140
  303.6 2.6 copy-start.2
  303.7 4.5 %collective-permute-start = (f32[32,512]{1,0:T(8,128)S(1)}, f32[32,512]{1,0:T(8,128)S(1)}, u32[]{:S(2)}, u32[]{:S(2)}) collective-permute-start(f32[32,512]{1,0:T(8,128)S(1)} %constant_dynamic-slice_fusion), channel_id=1, source_target_pairs={{0,32},{32,0},{64,96},{96,64},{128,160},{160,128},{192,224},{224,1... | collective-permute-start | bytes 196616 | tf_op jit(solution)/shard_map/ppermute | solution.py:38
Sparse Core Ops, SparseCore 0:
  80.4 32.2 all-gather.4
  114.8 39.9 all-gather.8
  156.9 40.9 all-gather.6
where the time goes:
time: 317 us; the launch traced here: 316 us
  blocking collectives  112 us (35%)
  waiting for transfers between devices  95.9 us (30%)
  matrix products  52.1 us (16%)
  starting transfers between devices  19.8 us (6%)
  between operations  16.2 us (5%)
  other arithmetic  10.6 us (3%)
  local copies, waits for them, and re-layouts  5.64 us (2%)
  loops' own time  3.56 us (1%)
    dot_general x24, matrix products, product(): jnp.dot(left, right, precision=lax.Precision.HIGHEST, preferred_element_t...  52.1 us
    psum x5, blocking collectives, by_axis(): return functools.reduce(lax.psum, axes, shard)  44 us
    all_to_all x1, blocking collectives, summed_on_arrival(): lax.all_to_all(tiles, axis, split_axis=0, concat_axis=0, tiled=True)  41.3 us
    all_gather x1, waiting for transfers between devices, local(): lax.all_gather(right_slab, REPLICA, axis=0, tiled=True)  35.6 us
    all_gather x1, waiting for transfers between devices, local(): lax.all_gather(grad_rows, REPLICA, axis=0, tiled=True)  31.6 us
    all_to_all x1, waiting for transfers between devices, sent_to_all(): lax.all_to_all(jnp.broadcast_to(shard[None], (count, *shard.shape)), axis...  28 us
    all_to_all x1, blocking collectives, local(): lax.all_to_all(ordered, MP, split_axis=1, concat_axis=0, tiled=True)  27.2 us
    all_to_all x1, starting transfers between devices, sent_to_all(): lax.all_to_all(jnp.broadcast_to(shard[None], (count, *shard.shape)), axis...  11 us
  transfers between devices with their start and end apart: 6, of which 3 were waited for; matrix products, arithmetic and copies ran while one was open for 20% of the time, Pallas kernels for 0%

commit v1 on v0

--- a/solution.py
+++ b/solution.py
@@ -109,7 +109,11 @@
     grad_rows = summed_on_arrival(routed.astype(jnp.float32), REPLICA, 0)
     folder = make_folder(grad_rows, left_slab, replica_index, rows_rep)
     left_term, right_term, half_dir = folder(
-        (zeros, zeros, zeros), lax.all_gather(grad_rows, REPLICA, axis=0, tiled=True), jnp.int32(0)
+        (zeros, zeros, zeros),
+        jnp.concatenate(
+            lax.all_to_all(jnp.stack([grad_rows] * lax.axis_size(REPLICA)), REPLICA, 0, 0), axis=0
+        ),
+        jnp.int32(0),
     )
     direction = product(half_dir, lax.all_gather(right_slab, REPLICA, axis=0, tiled=True))
     new_left = decay * left_stats[0] + (1.0 - decay) * left_term

time: 317 us -> 287 us (0.905)
  waiting for transfers between devices: 95.9 us -> 66.2 us
    all_gather x1 -> x0, waiting for transfers between devices: 31.6 us -> none  [local(): lax.all_gather(grad_rows, REPLICA, axis=0, tiled=True)]
    all_to_all x0 -> x1, waiting for transfers between devices: none -> 28.6 us  [local(): lax.all_to_all(jnp.stack([grad_rows] * lax.axis_size(REPLICA)), REPLICA,...]
    all_gather x1, waiting for transfers between devices: 35.6 us -> 9 us  [local(): lax.all_gather(right_slab, REPLICA, axis=0, tiled=True)]
    all_to_all x0 -> x1, starting transfers between devices: none -> 3.55 us  [local(): lax.all_to_all(jnp.stack([grad_rows] * lax.axis_size(REPLICA)), REPLICA,...]
  transfers between devices with their start and end apart: 6 -> 6, of which waited for: 3 -> 3; matrix products, arithmetic and copies ran while one was open for 20% -> 21% of each run, Pallas kernels for 0% -> 0%
where the time goes in v1:
time: 287 us; the launch traced here: 286 us
  blocking collectives  112 us (39%)
  waiting for transfers between devices  66.2 us (23%)
  matrix products  49.5 us (17%)
  starting transfers between devices  21.2 us (7%)
  between operations  16.4 us (6%)
  other arithmetic  9.95 us (3%)
  local copies, waits for them, and re-layouts  6.73 us (2%)
  loops' own time  3.69 us (1%)
    dot_general x24, matrix products, product(): jnp.dot(left, right, precision=lax.Precision.HIGHEST, preferred_element_t...  49.5 us
    psum x5, blocking collectives, by_axis(): return functools.reduce(lax.psum, axes, shard)  44.1 us
    all_to_all x1, blocking collectives, summed_on_arrival(): lax.all_to_all(tiles, axis, split_axis=0, concat_axis=0, tiled=True)  41.1 us
    all_to_all x1, waiting for transfers between devices, local(): lax.all_to_all(jnp.stack([grad_rows] * lax.axis_size(REPLICA)), REPLICA,...  28.6 us
    all_to_all x1, waiting for transfers between devices, sent_to_all(): lax.all_to_all(jnp.broadcast_to(shard[None], (count, *shard.shape)), axis...  28 us
    all_to_all x1, blocking collectives, local(): lax.all_to_all(ordered, MP, split_axis=1, concat_axis=0, tiled=True)  27.2 us
    all_to_all x1, starting transfers between devices, sent_to_all(): lax.all_to_all(jnp.broadcast_to(shard[None], (count, *shard.shape)), axis...  9.66 us
    all_gather x1, waiting for transfers between devices, local(): lax.all_gather(right_slab, REPLICA, axis=0, tiled=True)  9 us
  transfers between devices with their start and end apart: 6, of which 3 were waited for; matrix products, arithmetic and copies ran while one was open for 21% of the time, Pallas kernels for 0%

profile of v1, /device:TPU:1, one launch (start us, length us, event | category | flops | bytes accessed | tf_op | source)
XLA Modules:
  0.0 286.2 jit_solution(1271501867535731050)
XLA Ops:
  7.2 1.4 fusion.54
  8.7 1.2 copy.25
  10.9 27.2 %all_to_all.38 = bf16[32,16,512]{2,0,1:T(8,128)(2,1)S(1)} all-to-all(bf16[32,16,512]{2,0,1:T(8,128)(2,1)S(1)} %select_bitcast_fusion), channel_id=1, replica_groups=mesh['replica_0'=8,'replica_1'=2,'mp_0'=8,'mp_1'=2,'refresh'=2] {'mp_0',..., dimensions={1} | all-to-all | bytes 1048576 | tf_op jit(solution)/shard_map/all_to_all | solution.py:108
  38.2 41.1 %all_to_all.39 = f32[16,32,512]{2,1,0:T(8,128)S(1)} all-to-all(f32[16,32,512]{2,1,0:T(8,128)S(1)} %convert_bitcast_fusion), channel_id=1, replica_groups=mesh['replica_0'=8,'replica_1'=2,'mp_0'=8,'mp_1'=2,'refresh'=2] {'replic..., dimensions={0} | all-to-all | bytes 2097152 | tf_op jit(solution)/shard_map/all_to_all | solution.py:22
  79.4 1.1 stack.2
  80.5 3.6 %all-to-all-start.2 = ((f32[16,32,512]{2,1,0:T(8,128)}), f32[16,32,512]{2,1,0:T(8,128)S(1)}, u32[]{:S(2)}, u32[]{:S(2)}) async-start(f32[16,32,512]{2,1,0:T(8,128)} %stack.2), calls=%async_computation.2 | async-start | bytes 2097152 | tf_op jit(solution)/shard_map/all_to_all | solution.py:114
  84.2 0.7 all-gather.6.cloned.1.call-update
  84.9 28.6 %all-to-all-done.2 = f32[16,32,512]{2,1,0:T(8,128)S(1)} async-done(((f32[16,32,512]{2,1,0:T(8,128)}), f32[16,32,512]{2,1,0:T(8,128)S(1)}, u32[]{:S(2)}, u32[]{:S(2)}) %all-to-all-start.2) | async-done | bytes 1048608 | tf_op jit(solution)/shard_map/all_to_all | solution.py:114
  113.5 0.7 fusion.43
  114.2 1.0 fusion.42
  116.6 0.7 fusion.48
  117.4 9.0 %all-gather.6.cloned.1.call-done = f32[1,512,512]{2,1,0:T(8,128)} async-done(((f32[1,32,512]{2,1,0:T(8,128)}), f32[1,512,512]{2,1,0:T(8,128)}) %all-gather.6.cloned.1.call-update) | async-done | bytes 1048592 | tf_op jit(solution)/shard_map/all_gather | solution.py:118
  126.4 2.5 multiply_reduce_fusion.1
  128.9 13.5 %all-reduce.1 = (f32[]{:T(128)}, f32[]{:T(128)}) all-reduce(f32[]{:T(128)} %multiply_reduce_fusion.2, f32[]{:T(128)} %get-tuple-element.67), channel_id=1, replica_groups=mesh['replica_0'=8,'replica_1'=2,'mp_0'=8,'mp_1'=2,'refresh'=2] {'replic..., use_global_device_ids=true, to_apply=%region_3.4 | all-reduce | flops 2 | bytes 16 | tf_op jit(solution)/shard_map/psum | solution.py:27
  142.4 6.8 %all-reduce.4 = (f32[]{:T(128)}, f32[]{:T(128)}) all-reduce(f32[]{:T(128)} %get-tuple-element.55, f32[]{:T(128)} %get-tuple-element.56), channel_id=1, replica_groups=mesh['replica_0'=8,'replica_1'=2,'mp_0'=8,'mp_1'=2,'refresh'=2] {'replic..., use_global_device_ids=true, to_apply=%region_4.5 | all-reduce | flops 2 | bytes 16 | tf_op jit(solution)/shard_map/psum | solution.py:27
  149.2 13.5 %all-reduce = (f32[]{:T(128)}, f32[]{:T(128)}) all-reduce(f32[]{:T(128)} %get-tuple-element.61, f32[]{:T(128)} %get-tuple-element.62), channel_id=1, replica_groups=mesh['replica_0'=8,'replica_1'=2,'mp_0'=8,'mp_1'=2,'refresh'=2] {'mp_0'}, use_global_device_ids=true, to_apply=%region_5.6 | all-reduce | flops 2 | bytes 16 | tf_op jit(solution)/shard_map/psum | solution.py:27
  162.7 5.9 %all-reduce.3 = (f32[]{:T(128)}, f32[]{:T(128)}) all-reduce(f32[]{:T(128)} %get-tuple-element.53, f32[]{:T(128)} %get-tuple-element.54), channel_id=1, replica_groups=mesh['replica_0'=8,'replica_1'=2,'mp_0'=8,'mp_1'=2,'refresh'=2] {'mp_1'}, use_global_device_ids=true, to_apply=%region_6.7 | all-reduce | flops 2 | bytes 16 | tf_op jit(solution)/shard_map/psum | solution.py:27
  168.6 4.4 %all-reduce.2 = (f32[]{:T(128)}, f32[]{:T(128)}) all-reduce(f32[]{:T(128)} %get-tuple-element.59, f32[]{:T(128)} %get-tuple-element.60), channel_id=1, replica_groups=mesh['replica_0'=8,'replica_1'=2,'mp_0'=8,'mp_1'=2,'refresh'=2] {'refresh'}, use_global_device_ids=true, to_apply=%region_7.8 | all-reduce | flops 2 | bytes 16 | tf_op jit(solution)/shard_map/psum | solution.py:27
  174.4 1.1 broadcast_in_dim.66
  175.5 9.7 %all-to-all-start.3 = ((f32[16,32,512]{2,1,0:T(8,128)}), f32[16,32,512]{2,1,0:T(8,128)}, u32[]{:S(2)}, u32[]{:S(2)}) async-start(f32[16,32,512]{2,1,0:T(8,128)} %broadcast_in_dim.66), calls=%async_computation.3 | async-start | bytes 2097152 | tf_op jit(solution)/shard_map/all_to_all | solution.py:43
  185.3 28.0 %all-to-all-done.3 = f32[16,32,512]{2,1,0:T(8,128)} async-done(((f32[16,32,512]{2,1,0:T(8,128)}), f32[16,32,512]{2,1,0:T(8,128)}, u32[]{:S(2)}, u32[]{:S(2)}) %all-to-all-start.3) | async-done | bytes 1048608 | tf_op jit(solution)/shard_map/all_to_all | solution.py:43
  213.2 6.0 %all-to-all-start.4 = ((f32[16,32,512]{2,1,0:T(8,128)}), f32[16,32,512]{2,1,0:T(8,128)S(1)}, u32[]{:S(2)}, u32[]{:S(2)}) async-start(f32[16,32,512]{2,1,0:T(8,128)} %all-to-all-done.3), calls=%async_computation.4 | async-start | bytes 2097152 | tf_op jit(solution)/shard_map/all_to_all | solution.py:144
  219.3 2.4 multiply_reduce_fusion
  222.6 1.8 broadcast_multiply_fusion
  224.3 48.7 %while.13 = (s32[]{:T(128)}, f32[512,512]{0,1:T(8,128)S(1)}, f32[512,512]{1,0:T(8,128)S(1)}, s32[]{:T(128)}, s32[]{:T(128)}) while((s32[]{:T(128)}, f32[512,512]{0,1:T(8,128)S(1)}, f32[512,512]{1,0:T(8,128)S(1)}, s32[]{:T(128)}, s32[]{:T(128)}) %tuple.29), condition=%wide.region_17.18_spmd.clone, body=%wide.region_16.17_spmd.clone.sunk | while | flops 8058306560 | bytes 18874428 | solution.py:71
  225.3 3.5 %fusion.91 = f32[512,512]{1,0:T(8,128)S(1)} fusion(f32[512,512]{1,0:T(8,128)S(1)} %copy.39), kind=kOutput, calls=%fused_computation.10.clone.1 | convolution fusion | flops 1611661312 | bytes 2097152 | tf_op jit(solution)/shard_map/while/body/dot_general | solution.py:60
  228.8 1.9 fusion.92
  230.7 1.9 fusion.93
  232.6 1.9 convolution_bitcast_fusion.2
  234.6 1.9 fusion.94
  237.3 3.5 %fusion.91 = f32[512,512]{1,0:T(8,128)S(1)} fusion(f32[512,512]{1,0:T(8,128)S(1)} %copy.39), kind=kOutput, calls=%fused_computation.10.clone.1 | convolution fusion | flops 1611661312 | bytes 2097152 | tf_op jit(solution)/shard_map/while/body/dot_general | solution.py:60
  240.8 1.9 fusion.92
  242.7 1.9 fusion.93
  244.6 1.9 convolution_bitcast_fusion.2
  246.5 1.9 fusion.94
  249.2 3.5 %fusion.91 = f32[512,512]{1,0:T(8,128)S(1)} fusion(f32[512,512]{1,0:T(8,128)S(1)} %copy.39), kind=kOutput, calls=%fused_computation.10.clone.1 | convolution fusion | flops 1611661312 | bytes 2097152 | tf_op jit(solution)/shard_map/while/body/dot_general | solution.py:60
  252.7 1.9 fusion.92
  254.6 1.9 fusion.93
  256.6 1.9 convolution_bitcast_fusion.2
  258.5 1.9 fusion.94
  261.2 3.5 %fusion.91 = f32[512,512]{1,0:T(8,128)S(1)} fusion(f32[512,512]{1,0:T(8,128)S(1)} %copy.39), kind=kOutput, calls=%fused_computation.10.clone.1 | convolution fusion | flops 1611661312 | bytes 2097152 | tf_op jit(solution)/shard_map/while/body/dot_general | solution.py:60
  264.7 1.9 fusion.92
  266.6 1.9 fusion.93
  268.5 1.9 convolution_bitcast_fusion.2
  270.4 1.9 fusion.94
  273.4 1.9 collective-permute-start
  276.8 1.1 broadcast_select_fusion
  277.8 1.5 select_bitcast_fusion.1
  (50 shorter events, 5.3 us)
Async XLA Ops:
  7.2 109.4 %copy-start = (f32[1,32,512]{2,1,0:T(8,128)S(1)}, f32[1,32,512]{2,1,0:T(8,128)}, u32[]{:S(2)}) copy-start(f32[1,32,512]{2,1,0:T(8,128)} %param.12) | copy-start | bytes 196612
  79.4 34.1 %copy-start.4 = (f32[1,32,512]{2,1,0:T(8,128)S(1)}, f32[1,32,512]{2,1,0:T(8,128)}, u32[]{:S(2)}) copy-start(f32[1,32,512]{2,1,0:T(8,128)} %param.11) | copy-start | bytes 196612
  79.4 34.8 %copy-start.5 = (f32[1,32,512]{2,1,0:T(8,128)S(1)}, f32[1,32,512]{2,1,0:T(8,128)}, u32[]{:S(2)}) copy-start(f32[1,32,512]{2,1,0:T(8,128)} %param.10) | copy-start | bytes 196612
  80.5 32.9 %all-to-all-start.2 = ((f32[16,32,512]{2,1,0:T(8,128)}), f32[16,32,512]{2,1,0:T(8,128)S(1)}, u32[]{:S(2)}, u32[]{:S(2)}) async-start(f32[16,32,512]{2,1,0:T(8,128)} %stack.2), calls=%async_computation.2 | async-start | bytes 2097152 | tf_op jit(solution)/shard_map/all_to_all | solution.py:114
  84.1 42.2 %all-gather.6.cloned.1.call-start = ((), (), s32[]{:S(2)}) async-start(), calls=%async_computation.6 | async-start | bytes 1114112 | tf_op jit(solution)/shard_map/all_gather | solution.py:118
  84.8 134.4 %all-gather.4.cloned.1.call-start = ((), (), s32[]{:S(2)}) async-start(), calls=%async_computation.5 | async-start | bytes 2228224 | tf_op jit(solution)/shard_map/all_gather | solution.py:33
  114.2 60.1 %copy-start.2 = (f32[32,512]{1,0:T(8,128)}, f32[32,512]{1,0:T(8,128)S(1)}, u32[]{:S(2)}) copy-start(f32[32,512]{1,0:T(8,128)S(1)} %fusion.43) | copy-start | bytes 196612
  115.3 60.2 %copy-start.3 = (f32[32,512]{1,0:T(8,128)}, f32[32,512]{1,0:T(8,128)S(1)}, u32[]{:S(2)}) copy-start(f32[32,512]{1,0:T(8,128)S(1)} %fusion.42) | copy-start | bytes 196612
  117.3 67.9 %copy-start.6 = (s32[2,16]{1,0:T(2,128)S(1)}, s32[2,16]{1,0:T(2,128)}, u32[]{:S(2)}) copy-start(s32[2,16]{1,0:T(2,128)} %param.15) | copy-start | bytes 388
  175.5 37.8 %all-to-all-start.3 = ((f32[16,32,512]{2,1,0:T(8,128)}), f32[16,32,512]{2,1,0:T(8,128)}, u32[]{:S(2)}, u32[]{:S(2)}) async-start(f32[16,32,512]{2,1,0:T(8,128)} %broadcast_in_dim.66), calls=%async_computation.3 | async-start | bytes 2097152 | tf_op jit(solution)/shard_map/all_to_all | solution.py:43
  213.2 62.1 %all-to-all-start.4 = ((f32[16,32,512]{2,1,0:T(8,128)}), f32[16,32,512]{2,1,0:T(8,128)S(1)}, u32[]{:S(2)}, u32[]{:S(2)}) async-start(f32[16,32,512]{2,1,0:T(8,128)} %all-to-all-done.3), calls=%async_computation.4 | async-start | bytes 2097152 | tf_op jit(solution)/shard_map/all_to_all | solution.py:144
  273.3 2.6 copy-start.1
  273.4 4.5 %collective-permute-start = (f32[32,512]{1,0:T(8,128)S(1)}, f32[32,512]{1,0:T(8,128)S(1)}, u32[]{:S(2)}, u32[]{:S(2)}) collective-permute-start(f32[32,512]{1,0:T(8,128)S(1)} %constant_dynamic-slice_fusion), channel_id=1, source_target_pairs={{0,32},{32,0},{64,96},{96,64},{128,160},{160,128},{192,224},{224,1... | collective-permute-start | bytes 196616 | tf_op jit(solution)/shard_map/ppermute | solution.py:38
Sparse Core Ops, SparseCore 0:
  87.0 39.2 all-gather.5
  128.5 38.9 all-gather.3
